TPU v7x, 32 devices: a whole 2x2x4 slice. The times are simulated.
32 devices in a mesh: row: 4 (over y, core), col: 8 (over z, x).
Axes of the slice: x: 2, y: 2, z: 4, core: 2. Of those that a mesh axis runs over, the one named last changes fastest.
Arguments:
- singles: bfloat16 [96, 384], P(('row', 'col')), may hold values from -6 to 6
- pair: float32 [96, 96, 128], P('row', 'col'), may hold values from -48 to 48
- frames: float32 [96, 12], P(('row', 'col')), may hold values from -9 to 9, as said below
- w_query: bfloat16 [384, 336], replicated, may hold values from -0.3125 to 0.3125
- w_keyval: bfloat16 [384, 816], replicated, may hold values from -0.3125 to 0.3125
- w_bias: float32 [128, 12], replicated, may hold values from -1 to 1
- head_weights: float32 [12], replicated, may hold values from -2 to 1
- w_out: bfloat16 [2112, 384], replicated, may hold values from -0.125 to 0.125
Outputs:
- update: float32 [96, 384], P(('row', 'col'))
Inputs may be any that keep to these rules, and one draw needn't show every extreme that they name: `frames`: the first nine entries of a row are a rotation matrix in row-major order, the last three a translation.
All inputs are finite; a program needn't handle non-finite values.
Results may differ from a plain program's by a relative error of at most 0.0029.
Values sent between devices are 32-bit elements; how exact they have to be, the bound alone decides.
A program may use at most 64 MiB of HBM per device.

v0:
```python
import math
import jax
import jax.numpy as jnp
from jax import lax
from jax.sharding import PartitionSpec as P

CS = 384
CZ = 128
H = 12
CH = 16
PQ = 4
PV = 8
HIGHEST = lax.Precision.HIGHEST


def broadcast(value, axis, source):
    kept = jnp.where(lax.axis_index(axis) == source, value, 0).astype(value.dtype)
    return lax.psum(kept, axis)


def rigid_apply(frames, points):
    rotation = frames[:, :9].reshape(frames.shape[0], 3, 3)
    moved = jnp.einsum("nab,nbm->nam", rotation, points, precision=HIGHEST)
    return moved + frames[:, 9:12, None]


def query_side(singles, frames, w_query):
    row_count = singles.shape[0]
    scalar_width = H * CH
    projected = jnp.dot(singles, w_query, preferred_element_type=jnp.float32)
    points = rigid_apply(frames, projected[:, scalar_width:].reshape(row_count, 3, H * PQ))
    return jnp.concatenate([projected[:, :scalar_width], points.reshape(row_count, 3 * H * PQ)], 1)


def key_side(singles, frames, w_keyval):
    row_count = singles.shape[0]
    scalar_width = 2 * H * CH
    point_end = scalar_width + 3 * H * PQ
    projected = jnp.dot(singles, w_keyval, preferred_element_type=jnp.float32)
    key_points = rigid_apply(
        frames, projected[:, scalar_width:point_end].reshape(row_count, 3, H * PQ)
    )
    value_points = rigid_apply(frames, projected[:, point_end:].reshape(row_count, 3, H * PV))
    return jnp.concatenate(
        [
            projected[:, :scalar_width],
            key_points.reshape(row_count, 3 * H * PQ),
            value_points.reshape(row_count, 3 * H * PV),
        ],
        1,
    )


def logits_of(query_feat, key_feat, pair_block, w_bias, head_weights):
    query_rows = query_feat.shape[0]
    key_rows = key_feat.shape[0]
    scalar_width = H * CH
    query_vec = query_feat[:, :scalar_width].reshape(query_rows, H, CH)
    query_points = query_feat[:, scalar_width:].reshape(query_rows, 3, H, PQ)
    key_vec = key_feat[:, :scalar_width].reshape(key_rows, H, CH)
    key_points = key_feat[:, 2 * scalar_width : 2 * scalar_width + 3 * H * PQ].reshape(
        key_rows, 3, H, PQ
    )
    scalar = jnp.einsum("ihc,jhc->ihj", query_vec, key_vec, precision=HIGHEST) / math.sqrt(CH)
    pair_bias = jnp.einsum("ijc,ch->ihj", pair_block, w_bias, precision=HIGHEST)
    cross_term = jnp.einsum("iahp,jahp->ihj", query_points, key_points, precision=HIGHEST)
    query_square = jnp.sum(query_points * query_points, axis=(1, 3))
    key_square = jnp.sum(key_points * key_points, axis=(1, 3))
    distance = query_square[:, :, None] + key_square.T[None, :, :] - 2.0 * cross_term
    weight = jax.nn.softplus(head_weights) * (math.sqrt(2.0 / (9.0 * PQ)) / 2.0)
    return math.sqrt(1.0 / 3.0) * (scalar + pair_bias - weight[None, :, None] * distance)


def weighted(exponent, key_feat, pair_block):
    key_rows = key_feat.shape[0]
    scalar_width = H * CH
    value_vec = key_feat[:, scalar_width : 2 * scalar_width].reshape(key_rows, H, CH)
    value_points = key_feat[:, 2 * scalar_width + 3 * H * PQ :].reshape(key_rows, 3, H, PV)
    weight_sum = jnp.sum(exponent, axis=2)
    scalar = jnp.einsum("ihj,jhc->ihc", exponent, value_vec, precision=HIGHEST)
    points = jnp.einsum("ihj,jahp->iahp", exponent, value_points, precision=HIGHEST)
    paired = jnp.einsum("ihj,ijc->ihc", exponent, pair_block, precision=HIGHEST)
    return (weight_sum, scalar, points, paired)


def finish_rest(scalar, points, frames, w_out):
    row_count = scalar.shape[0]
    rotation = frames[:, :9].reshape(row_count, 3, 3)
    relative = points - frames[:, 9:12, None, None]
    local_points = jnp.einsum("nba,nbhp->nahp", rotation, relative, precision=HIGHEST)
    length = jnp.sqrt(jnp.sum(local_points * local_points, axis=1) + 1.0)
    features = jnp.concatenate(
        [
            scalar.reshape(row_count, H * CH),
            local_points.reshape(row_count, 3 * H * PV),
            length.reshape(row_count, H * PV),
        ],
        1,
    )
    features = features.astype(jnp.bfloat16)
    return jnp.dot(features, w_out[: H * (CH + 4 * PV)], preferred_element_type=jnp.float32)


def paired_term(paired, w_out):
    row_count = paired.shape[0]
    pair_rows = w_out[H * (CH + 4 * PV) :].astype(jnp.float32)
    return jnp.dot(paired.reshape(row_count, H * CZ), pair_rows, precision=HIGHEST)


def finish(weight_sum, scalar, points, paired, frames, w_out):
    scalar = scalar / weight_sum[:, :, None]
    points = points / weight_sum[:, None, :, None]
    paired = paired / weight_sum[:, :, None]
    return finish_rest(scalar, points, frames, w_out) + paired_term(paired, w_out)


def block_size(total):
    chosen_size = 1
    for candidate in range(1, min(total, 32) + 1):
        if total % candidate == 0:
            chosen_size = candidate
    return chosen_size


def by_blocks(compute, arrays, total):
    size = block_size(total)
    count = total // size

    def one_block(start):
        pieces = [lax.dynamic_slice_in_dim(array, start, size, 0) for array in arrays]
        return compute(*pieces)

    starts = jnp.arange(count) * size
    results = lax.map(one_block, starts)
    return jax.tree.map(lambda value: value.reshape((total,) + value.shape[2:]), results)


def blocked_logits(query_feat, key_feat, pair, w_bias, head_weights):

    def compute(query_part, pair_part):
        return logits_of(query_part, key_feat, pair_part, w_bias, head_weights)

    return by_blocks(compute, [query_feat, pair], pair.shape[0])


def blocked_weighted(logits, shift, key_feat, pair):

    def compute(logit_part, shift_part, pair_part):
        return weighted(jnp.exp(logit_part - shift_part[:, :, None]), key_feat, pair_part)

    return by_blocks(compute, [logits, shift, pair], pair.shape[0])


def body(singles, pair, frames, w_query, w_keyval, w_bias, head_weights, w_out):
    rows_dev = singles.shape[0]
    query_rows = pair.shape[0]
    key_rows = pair.shape[1]
    column = lax.axis_index("col")
    ratio = query_rows // key_rows
    source = column // ratio
    within = column % ratio * key_rows
    packed = jnp.concatenate([singles.astype(jnp.float32), frames], 1)
    row_packed = lax.all_gather(packed, "col", axis=0, tiled=True)
    chosen = lax.dynamic_slice_in_dim(row_packed, within, key_rows, 0)
    arrived = broadcast(chosen, "row", source)
    query_feat = query_side(row_packed[:, :CS].astype(jnp.bfloat16), row_packed[:, CS:], w_query)
    key_feat = key_side(arrived[:, :CS].astype(jnp.bfloat16), arrived[:, CS:], w_keyval)
    logits = blocked_logits(query_feat, key_feat, pair, w_bias, head_weights)
    local_peak = jnp.max(logits, axis=2)
    own_start = column * rows_dev
    peak = lax.pmax(local_peak, "col")
    part_sum, part_scalar, part_points, part_paired = blocked_weighted(logits, peak, key_feat, pair)
    summed = lax.psum((part_sum, part_scalar, part_points, part_paired), "col")
    weight_sum, scalar, points, paired = [
        lax.dynamic_slice_in_dim(piece, own_start, rows_dev, 0) for piece in summed
    ]
    return finish(weight_sum, scalar, points, paired, frames, w_out)


def solution(mesh):
    return jax.shard_map(
        body,
        mesh=mesh,
        in_specs=(
            P(("row", "col"), None),
            P("row", "col", None),
            P(("row", "col"), None),
            P(),
            P(),
            P(),
            P(),
            P(),
        ),
        out_specs=P(("row", "col"), None),
        check_vma=False,
    )
```

profile of v0, /device:TPU:0, one launch (start us, length us, event | category | flops | bytes accessed | tf_op | source)
XLA Modules:
  0.0 156.1 jit_solution(14814837688478335846)
XLA Ops:
  6.5 0.0 copy-start
  6.5 0.0 all-reduce.3.cloned.1.call-start
  6.6 0.7 convert_element_type.4
  7.3 0.7 maximum_bitcast_fusion
  8.0 32.3 %all-gather = f32[8,3,396]{2,1,0:T(4,128)S(1)} all-gather(f32[1,3,396]{2,1,0:T(4,128)S(1)} %maximum_bitcast_fusion), channel_id=1, replica_groups=mesh['row'=4,'col'=8] {'col'}, dimensions={0}, use_global_device_ids=true | all-gather | bytes 42768 | tf_op jit(solution)/shard_map/all_gather | solution.py:163
  40.5 10.3 %psum.35 = f32[12,396]{1,0:T(8,128)S(1)} all-reduce(f32[12,396]{1,0:T(8,128)S(1)} %dynamic-slice_select_fusion), channel_id=1, replica_groups=mesh['row'=4,'col'=8] {'row'}, use_global_device_ids=true, to_apply=%region_0.1 | all-reduce | flops 4752 | bytes 38016 | tf_op jit(solution)/shard_map/psum | solution.py:18
  50.7 0.1 slice.93
  50.8 0.1 slice.90
  50.9 1.1 fusion.22
  52.0 0.1 slice.89
  52.1 0.0 copy-done
  52.1 0.3 fusion.23
  52.4 0.1 fusion.36
  52.5 0.1 reshape.95
  52.6 0.1 reshape.81
  52.6 0.2 multiply_reduce_fusion.2
  52.9 0.1 copy.56
  53.0 0.1 reshape.94
  53.1 0.1 reshape.79
  53.2 0.3 multiply_reduce_fusion.1
  53.5 0.1 copy.57
  53.6 0.1 copy.55
  53.7 0.1 copy.52
  53.8 0.0 copy-done.5
  53.9 0.1 copy.47
  54.0 0.1 reshape.76
  54.1 0.0 copy-done.2
  54.1 0.0 copy-done.4
  54.1 0.8 fusion.24
  54.9 0.4 fusion.9
  55.3 0.3 fusion.37
  55.6 21.6 %pmax.7 = f32[24,12]{0,1:T(8,128)S(1)} all-reduce(f32[24,12]{0,1:T(8,128)S(1)} %get-tuple-element.60), channel_id=1, replica_groups=mesh['row'=4,'col'=8] {'col'}, use_global_device_ids=true, to_apply=%region_6.7 | all-reduce | flops 288 | bytes 2304 | tf_op jit(solution)/shard_map/pmax | solution.py:171
  77.2 0.2 copy.68
  77.4 0.0 copy-start.1
  77.4 1.0 fusion.15
  78.4 0.0 all-reduce.3.cloned.1.call-update
  78.4 0.1 slice.94
  78.5 0.0 copy-done.3
  78.5 0.1 slice.79
  78.6 0.1 reshape.84
  78.6 0.2 convolution_add_fusion.1
  78.9 0.1 copy.60
  79.0 0.4 convolution_bitcast_fusion
  79.4 0.1 copy.73
  79.5 0.2 convolution_bitcast_fusion.1
  79.7 0.1 copy.62
  79.8 36.4 %all-reduce = (f32[24,3,12,8]{0,3,1,2:T(8,128)S(1)}, f32[24,12]{0,1:T(8,128)S(1)}, f32[24,12,16]{0,2,1:T(8,128)S(1)}) all-reduce(f32[24,3,12,8]{0,3,1,2:T(8,128)S(1)} %convolution_bitcast_fusion, f32[24,12]{0,1:T(8,128)S(1)} %get-tuple-element.40, ...), channel_id=1, replica_groups=mesh['row'=4,'col'=8] {'col'}, use_global_device_ids=true, to_apply=%region_10.11 | all-reduce | flops 11808 | bytes 94464 | tf_op jit(solution)/shard_map/psum | solution.py:173
  116.2 0.1 constant_dynamic-slice_fusion
  116.3 0.1 copy.70
  116.4 0.1 divide_subtract_fusion
  116.5 0.3 copy.63
  116.8 0.1 reshape.85
  116.9 0.3 convert_bitcast_fusion
  117.2 0.1 copy.66
  117.3 0.1 sqrt.8
  117.4 0.1 copy.65
  117.6 0.1 reshape.86
  117.7 0.1 divide_convert_fusion
  117.8 0.1 copy.67
  117.9 0.0 copy-done.1
  117.9 0.2 fusion.13
  118.1 29.1 %all-reduce.3.cloned.1.call-done = f32[24,12,128]{2,1,0:T(8,128)} async-done(((f32[24,12,128]{2,1,0:T(8,128)}), f32[24,12,128]{2,1,0:T(8,128)}) %all-reduce.3.cloned.1.call-update) | async-done | bytes 147472 | tf_op jit(solution)/shard_map/psum | solution.py:173
  147.2 0.8 divide_bitcast_fusion
  148.1 1.2 fusion.10
  (15 shorter events, 0.2 us)
Async XLA Ops:
  6.5 45.6 %copy-start = (bf16[384,816]{0,1:T(8,128)(2,1)S(1)}, bf16[384,816]{0,1:T(8,128)(2,1)}, u32[]{:S(2)}) copy-start(bf16[384,816]{0,1:T(8,128)(2,1)} %param.12) | copy-start | bytes 1880068
  6.5 47.3 %copy-start.5 = (f32[12]{0:T(128)S(1)}, f32[12]{0:T(128)}, u32[]{:S(2)}) copy-start(f32[12]{0:T(128)} %param.14) | copy-start | bytes 148
  6.5 47.5 %copy-start.2 = (f32[24,12,128]{2,0,1:T(8,128)S(1)}, f32[24,12,128]{2,0,1:T(8,128)}, u32[]{:S(2)}) copy-start(f32[24,12,128]{2,0,1:T(8,128)} %param.9) | copy-start | bytes 442372
  6.5 47.5 %copy-start.4 = (f32[128,12]{0,1:T(8,128)S(1)}, f32[128,12]{0,1:T(8,128)}, u32[]{:S(2)}) copy-start(f32[128,12]{0,1:T(8,128)} %param.13) | copy-start | bytes 18436
  6.5 140.7 %all-reduce.3.cloned.1.call-start = ((), (), s32[]{:S(2)}) async-start(), calls=%async_computation | async-start | bytes 393216 | tf_op jit(solution)/shard_map/psum | solution.py:173
  53.0 25.5 %copy-start.3 = (f32[3,12]{1,0:T(4,128)S(1)}, f32[3,12]{1,0:T(4,128)}, u32[]{:S(2)}) copy-start(f32[3,12]{1,0:T(4,128)} %param.10) | copy-start | bytes 436
  77.4 40.5 %copy-start.1 = (bf16[2112,384]{1,0:T(8,128)(2,1)S(1)}, bf16[2112,384]{1,0:T(8,128)(2,1)}, u32[]{:S(2)}) copy-start(bf16[2112,384]{1,0:T(8,128)(2,1)} %param.15) | copy-start | bytes 4866052
Sparse Core Ops, SparseCore 0:
  78.5 68.6 all-reduce.2
where the time goes:
time: 156 us
  blocking collectives  101 us (65%)
  waiting for transfers between devices  29.1 us (19%)
  between operations  13.7 us (9%)
  matrix products  6.99 us (4%)
  local copies, waits for them, and re-layouts  3.08 us (2%)
  other arithmetic  2.58 us (2%)
    psum x1, blocking collectives, body(): summed = lax.psum((part_sum, part_scalar, part_points, part_paired), 'col')  36.4 us
    all_gather x1, blocking collectives, body(): row_packed = lax.all_gather(packed, 'col', axis=0, tiled=True)  32.3 us
    psum x1, waiting for transfers between devices, body(): summed = lax.psum((part_sum, part_scalar, part_points, part_paired), 'col')  29.1 us
    pmax x1, blocking collectives, body(): peak = lax.pmax(local_peak, 'col')  21.6 us
    psum x1, blocking collectives, broadcast(): return lax.psum(kept, axis)  10.3 us
  transfers between devices with their start and end apart: 1, of which 1 were waited for; matrix products, arithmetic and copies ran while one was open for 2% of the time, Pallas kernels for 0%

commit v1 on v0

--- a/solution.py
+++ b/solution.py
@@ -13,9 +13,15 @@
 HIGHEST = lax.Precision.HIGHEST
 
 
+def gather_and_add(x, name):
+    parts = lax.all_gather(x, name, axis=0, tiled=False)
+    total = parts.sum(axis=0)
+    return total
+
+
 def broadcast(value, axis, source):
     kept = jnp.where(lax.axis_index(axis) == source, value, 0).astype(value.dtype)
-    return lax.psum(kept, axis)
+    return gather_and_add(kept, axis)
 
 
 def rigid_apply(frames, points):

time: 156 us -> 151 us (0.968)
  blocking collectives: 101 us -> 95.4 us
    psum x1 -> x0, blocking collectives: 10.3 us -> none  [broadcast(): return lax.psum(kept, axis)]
    all_gather x0 -> x1, blocking collectives: none -> 5.42 us  [gather_and_add(): parts = lax.all_gather(x, name, axis=0, tiled=False)]
where the time goes in v1:
time: 151 us
  blocking collectives  95.4 us (63%)
  waiting for transfers between devices  29 us (19%)
  between operations  13.7 us (9%)
  matrix products  6.99 us (5%)
  local copies, waits for them, and re-layouts  3.07 us (2%)
  other arithmetic  2.59 us (2%)
    psum x1, blocking collectives, body(): summed = lax.psum((part_sum, part_scalar, part_points, part_paired), 'col')  36.1 us
    all_gather x1, blocking collectives, body(): row_packed = lax.all_gather(packed, 'col', axis=0, tiled=True)  32.3 us
    psum x1, waiting for transfers between devices, body(): summed = lax.psum((part_sum, part_scalar, part_points, part_paired), 'col')  29 us
    pmax x1, blocking collectives, body(): peak = lax.pmax(local_peak, 'col')  21.6 us
    all_gather x1, blocking collectives, gather_and_add(): parts = lax.all_gather(x, name, axis=0, tiled=False)  5.42 us
  transfers between devices with their start and end apart: 1, of which 1 were waited for; matrix products, arithmetic and copies ran while one was open for 2% of the time, Pallas kernels for 0%

profile of v1, /device:TPU:0, one launch (start us, length us, event | category | flops | bytes accessed | tf_op | source)
XLA Modules:
  0.0 150.8 jit_solution(12357624864383781855)
XLA Ops:
  6.5 0.0 copy-start
  6.5 0.0 all-reduce.3.cloned.1.call-start
  6.6 0.7 convert_element_type.4
  7.3 0.7 maximum_bitcast_fusion
  8.0 32.3 %all-gather.1 = f32[8,3,396]{2,1,0:T(4,128)S(1)} all-gather(f32[1,3,396]{2,1,0:T(4,128)S(1)} %maximum_bitcast_fusion), channel_id=1, replica_groups=mesh['row'=4,'col'=8] {'col'}, dimensions={0}, use_global_device_ids=true | all-gather | bytes 42768 | tf_op jit(solution)/shard_map/all_gather | solution.py:169
  40.5 5.4 %all-gather.2 = f32[4,12,396]{2,1,0:T(8,128)S(1)} all-gather(f32[1,12,396]{2,1,0:T(8,128)S(1)} %select_bitcast_fusion), channel_id=2, replica_groups=mesh['row'=4,'col'=8] {'row'}, dimensions={0}, use_global_device_ids=true | all-gather | bytes 95040 | tf_op jit(solution)/shard_map/all_gather | solution.py:17
  45.9 0.1 slice.93
  46.0 0.1 slice.90
  46.0 1.1 fusion.22
  47.2 0.1 slice.89
  47.3 0.0 copy-done
  47.3 0.3 fusion.23
  47.6 0.1 fusion.36
  47.6 0.1 reshape.99
  47.7 0.1 reshape.81
  47.8 0.2 multiply_reduce_fusion.2
  48.1 0.1 copy.56
  48.2 0.1 reshape.98
  48.3 0.1 reshape.79
  48.3 0.3 multiply_reduce_fusion.1
  48.7 0.1 copy.57
  48.8 0.1 copy.55
  48.9 0.1 copy.52
  49.0 0.0 copy-done.5
  49.0 0.1 copy.47
  49.1 0.1 reshape.76
  49.2 0.0 copy-done.2
  49.2 0.0 copy-done.4
  49.2 0.8 fusion.24
  50.1 0.4 fusion.9
  50.5 0.3 fusion.37
  50.7 21.6 %pmax.7 = f32[24,12]{0,1:T(8,128)S(1)} all-reduce(f32[24,12]{0,1:T(8,128)S(1)} %get-tuple-element.60), channel_id=1, replica_groups=mesh['row'=4,'col'=8] {'col'}, use_global_device_ids=true, to_apply=%region_6.7 | all-reduce | flops 288 | bytes 2304 | tf_op jit(solution)/shard_map/pmax | solution.py:177
  72.3 0.2 copy.68
  72.5 0.0 copy-start.1
  72.5 1.0 fusion.15
  73.5 0.0 all-reduce.3.cloned.1.call-update
  73.6 0.1 slice.94
  73.6 0.0 copy-done.3
  73.6 0.1 slice.79
  73.7 0.1 reshape.84
  73.8 0.2 convolution_add_fusion.1
  74.0 0.1 copy.60
  74.2 0.4 convolution_bitcast_fusion
  74.5 0.1 copy.73
  74.6 0.2 convolution_bitcast_fusion.1
  74.9 0.1 copy.62
  75.0 36.1 %all-reduce = (f32[24,3,12,8]{0,3,1,2:T(8,128)S(1)}, f32[24,12]{0,1:T(8,128)S(1)}, f32[24,12,16]{0,2,1:T(8,128)S(1)}) all-reduce(f32[24,3,12,8]{0,3,1,2:T(8,128)S(1)} %convolution_bitcast_fusion, f32[24,12]{0,1:T(8,128)S(1)} %get-tuple-element.40, ...), channel_id=1, replica_groups=mesh['row'=4,'col'=8] {'col'}, use_global_device_ids=true, to_apply=%region_10.11 | all-reduce | flops 11808 | bytes 94464 | tf_op jit(solution)/shard_map/psum | solution.py:179
  111.1 0.1 constant_dynamic-slice_fusion
  111.1 0.1 copy.70
  111.2 0.1 divide_subtract_fusion
  111.4 0.3 copy.63
  111.7 0.1 reshape.85
  111.8 0.3 convert_bitcast_fusion
  112.1 0.1 copy.66
  112.2 0.1 sqrt.8
  112.3 0.1 copy.65
  112.5 0.1 reshape.86
  112.6 0.1 divide_convert_fusion
  112.7 0.1 copy.67
  112.8 0.0 copy-done.1
  112.8 0.2 fusion.13
  113.0 29.0 %all-reduce.3.cloned.1.call-done = f32[24,12,128]{2,1,0:T(8,128)} async-done(((f32[24,12,128]{2,1,0:T(8,128)}), f32[24,12,128]{2,1,0:T(8,128)}) %all-reduce.3.cloned.1.call-update) | async-done | bytes 147472 | tf_op jit(solution)/shard_map/psum | solution.py:179
  142.0 0.8 divide_bitcast_fusion
  142.8 1.2 fusion.10
  (16 shorter events, 0.2 us)
Async XLA Ops:
  6.5 40.7 %copy-start = (bf16[384,816]{0,1:T(8,128)(2,1)S(1)}, bf16[384,816]{0,1:T(8,128)(2,1)}, u32[]{:S(2)}) copy-start(bf16[384,816]{0,1:T(8,128)(2,1)} %param.12) | copy-start | bytes 1880068
  6.5 42.5 %copy-start.5 = (f32[12]{0:T(128)S(1)}, f32[12]{0:T(128)}, u32[]{:S(2)}) copy-start(f32[12]{0:T(128)} %param.14) | copy-start | bytes 148
  6.5 42.7 %copy-start.2 = (f32[24,12,128]{2,0,1:T(8,128)S(1)}, f32[24,12,128]{2,0,1:T(8,128)}, u32[]{:S(2)}) copy-start(f32[24,12,128]{2,0,1:T(8,128)} %param.9) | copy-start | bytes 442372
  6.5 42.7 %copy-start.4 = (f32[128,12]{0,1:T(8,128)S(1)}, f32[128,12]{0,1:T(8,128)}, u32[]{:S(2)}) copy-start(f32[128,12]{0,1:T(8,128)} %param.13) | copy-start | bytes 18436
  6.5 135.4 %all-reduce.3.cloned.1.call-start = ((), (), s32[]{:S(2)}) async-start(), calls=%async_computation | async-start | bytes 393216 | tf_op jit(solution)/shard_map/psum | solution.py:179
  48.2 25.5 %copy-start.3 = (f32[3,12]{1,0:T(4,128)S(1)}, f32[3,12]{1,0:T(4,128)}, u32[]{:S(2)}) copy-start(f32[3,12]{1,0:T(4,128)} %param.10) | copy-start | bytes 436
  72.5 40.2 %copy-start.1 = (bf16[2112,384]{1,0:T(8,128)(2,1)S(1)}, bf16[2112,384]{1,0:T(8,128)(2,1)}, u32[]{:S(2)}) copy-start(bf16[2112,384]{1,0:T(8,128)(2,1)} %param.15) | copy-start | bytes 4866052
Sparse Core Ops, SparseCore 0:
  73.7 68.2 all-reduce.2
